TPU v7x, 128 devices: a whole 4x4x4 slice. The times are simulated.
128 devices in a mesh: aux: 8 (over z, core), orb: 16 (over x, y).
Axes of the slice: x: 4, y: 4, z: 4, core: 2. Of those that a mesh axis runs over, the one named last changes fastest.
Arguments:
- half: bfloat16 [128, 384, 3072], P('aux', 'orb'), may hold values from -1 to 1
- metric: bfloat16 [128, 128], P('aux'), may hold values from -1 to 2
- survive: int32 [8, 16, 24], P('aux', 'orb'), may hold values 0 or 1
Outputs:
- exchange_k: float32 [3072, 3072], P('orb', 'aux')
All inputs are finite; a program needn't handle non-finite values. No bound on the sum of `survive` on one device may be relied on, other than what follows from the above.
Results may differ from a plain program's by a relative error of at most 0.00098.
Values may be sent and summed in bfloat16 or wider, within the bound.
A program may use at most 128 MiB of HBM per device.

v0:
```python
import functools

import jax
import jax.numpy as jnp
from jax import lax
from jax.experimental import pallas as pl
from jax.experimental.pallas import tpu as pltpu
from jax.sharding import PartitionSpec as P

MESH = pl.DeviceIdType.MESH
F32 = jnp.float32


def gated(half, survive):
    aux_local, occ_local, ao_count = half.shape
    blocks_aux, blocks_occ, blocks_ao = survive.shape
    gate = survive.astype(jnp.bfloat16)
    shaped = half.reshape(
        blocks_aux, aux_local, blocks_occ, occ_local // blocks_occ, blocks_ao, ao_count // blocks_ao
    )
    return (shaped * gate[:, None, :, None, :, None]).reshape(aux_local, occ_local, ao_count)


def plain(half, metric, survive):
    aux_local, occ_local, ao_count = half.shape
    portion = lax.all_gather(gated(half, survive), "aux", axis=0, tiled=True)
    fit_total = jnp.dot(metric, portion.reshape(portion.shape[0], -1), preferred_element_type=F32)
    fitted = fit_total.astype(jnp.bfloat16).reshape(aux_local, occ_local, ao_count)
    group_width = ao_count // lax.axis_size("orb")
    row_start = lax.axis_index("orb") * group_width
    flat_rows = lax.all_gather(fitted, "orb", axis=1, tiled=True).reshape(-1, ao_count)
    left_rows = lax.dynamic_slice_in_dim(flat_rows, row_start, group_width, 1)
    partial_k = lax.dot_general(
        left_rows, flat_rows, (((0,), (0,)), ((), ())), preferred_element_type=F32
    )
    return lax.psum_scatter(partial_k, "aux", scatter_dimension=1, tiled=True)


def kernel(
    aux_local, m_ref, metric_ref, out_ref, held, fit, left, acc, peer, tile, via, last, whole, kron_ref,
    gs, gr, zs, zr, xs, xr, ys, yr, fs, fr, ps, pr, rs, rr,
):
    z = lax.axis_index("aux")
    orb = lax.axis_index("orb")
    n_aux = m_ref.shape[0]
    unit = m_ref.shape[1]
    ao = m_ref.shape[2]
    chip = orb // 2
    core = orb % 2
    pair_rows = acc.shape[0]
    rows = pair_rows // 2
    cols = out_ref.shape[1]
    half_rows = rows // 2
    x_peer = orb + 2 - 4 * (chip % 2)
    y_peer = orb + 4 - 8 * (chip // 2)
    partner = orb + 1 - 2 * core
    up, down, far = (z + 1) % n_aux, (z + n_aux - 1) % n_aux, (z + 2) % n_aux

    barrier = pltpu.get_barrier_semaphore()
    for a in (up, down, far):
        pl.semaphore_signal(barrier, inc=1, device_id={"aux": a, "orb": orb}, device_id_type=MESH)
    for o in (x_peer, y_peer, partner):
        pl.semaphore_signal(barrier, inc=1, device_id={"aux": z, "orb": o}, device_id_type=MESH)
    pl.semaphore_wait(barrier, 6)

    def remote(src, dst, send, recv, a, o):
        return pltpu.make_async_remote_copy(
            src_ref=src, dst_ref=dst, send_sem=send, recv_sem=recv,
            device_id={"aux": a, "orb": o}, device_id_type=MESH,
        )

    def span(s):
        return pl.ds(pl.multiple_of(s * unit, unit), unit)

    def source(d):
        return (z + n_aux - d) % n_aux

    metric_rows = pl.ds(pl.multiple_of(z * aux_local, aux_local), aux_local)
    gather = []
    for d in (1, 3, 2):
        copy = remote(metric_ref, whole.at[metric_rows], gs.at[d], gr.at[d], (z + d) % n_aux, orb)
        copy.start()
        gather.append(copy)
    spread = {}
    for d in (1, 3, 2):
        there = (z + d) % n_aux
        spread[d] = remote(m_ref.at[there], held.at[0, span(z)], zs.at[d], zr.at[d], there, orb)
        spread[d].start()

    to_x, to_y, onward = {}, {}, {}

    def share(d):
        own = span(source(d))
        if d:
            spread[d].wait_recv()
        block = held.at[0, own] if d else m_ref.at[z]
        to_x[d] = remote(block, held.at[1, own], xs.at[d], xr.at[d], z, x_peer)
        to_y[d] = remote(block, held.at[2, own], ys.at[d], yr.at[d], z, y_peer)
        to_x[d].start()
        to_y[d].start()

    def forward(d, from_x):
        own = span(source(d))
        if from_x:
            to_x[d].wait_recv()
            onward[d] = remote(held.at[1, own], held.at[3, own], fs.at[d], fr.at[d], z, y_peer)
        else:
            to_y[d].wait_recv()
            onward[d] = remote(held.at[2, own], held.at[3, own], fs.at[d], fr.at[d], z, x_peer)
        onward[d].start()

    step = 512
    mine = pl.ds(pl.multiple_of(chip * pair_rows, pair_rows), pair_rows)

    def contract(slot, first):
        @pl.loop(0, ao // step)
        def _(t):
            at = pl.ds(pl.multiple_of(t * step, step), step)
            fit[:, at] = jnp.dot(
                kron_ref[...], held[slot, :, at], preferred_element_type=F32
            ).astype(fit.dtype)

        left[...] = fit[:, mine].T

        @pl.loop(0, ao // step)
        def _(t):
            at = pl.ds(pl.multiple_of(t * step, step), step)
            more = jnp.dot(left[...], fit[:, at], preferred_element_type=F32)
            acc[:, at] = more if first else acc[:, at] + more

    def build_kron():
        whole[metric_rows, :] = metric_ref[...]
        for copy in gather:
            copy.wait_recv()
        depth, width = kron_ref.shape[0], whole.shape[1]

        def aux_of(r):
            return lax.div(r, unit) * aux_local + lax.rem(r, aux_local)

        def orbital_of(r):
            return lax.div(lax.rem(r, unit), aux_local)

        i32, bf16 = jnp.int32, kron_ref.dtype
        by_row = aux_of(lax.broadcasted_iota(i32, (width, depth), 1))
        pick = jnp.where(by_row == lax.broadcasted_iota(i32, (width, depth), 0), 1.0, 0.0)
        spread_cols = jnp.dot(whole[...], pick.astype(bf16), preferred_element_type=F32).astype(bf16)
        by_col = aux_of(lax.broadcasted_iota(i32, (depth, whole.shape[0]), 0))
        take = jnp.where(by_col == lax.broadcasted_iota(i32, (depth, whole.shape[0]), 1), 1.0, 0.0)
        both = jnp.dot(take.astype(bf16), spread_cols, preferred_element_type=F32)
        same = orbital_of(lax.broadcasted_iota(i32, (depth, depth), 0)) == orbital_of(
            lax.broadcasted_iota(i32, (depth, depth), 1)
        )
        kron_ref[...] = jnp.where(same, both, 0.0).astype(bf16)

    share(0)
    held[0, span(z), :] = m_ref[z]
    build_kron()
    share(1)
    share(3)
    forward(0, True)
    share(2)
    forward(1, False)
    contract(0, True)
    forward(3, True)
    to_x[1].wait_recv()
    to_x[2].wait_recv()
    contract(1, False)
    forward(2, False)
    to_y[0].wait_recv()
    to_y[3].wait_recv()
    contract(2, False)
    for d in range(4):
        onward[d].wait_recv()
    contract(3, False)

    def across(a):
        return pl.ds(pl.multiple_of(a * cols, cols), cols)

    my_rows = pl.ds(pl.multiple_of(core * rows, rows), rows)
    other_rows = pl.ds(pl.multiple_of((1 - core) * rows, rows), rows)
    order = (far, up, down, z)
    swaps = []
    for n, a in enumerate(order):
        swap = remote(acc.at[other_rows, across(a)], peer.at[n], ps.at[n], pr.at[n], z, partner)
        swap.start()
        swaps.append(swap)

    low, high = pl.ds(0, half_rows), pl.ds(half_rows, half_rows)

    def settle(n):
        swaps[n].wait_recv()
        tile[n] = acc[my_rows, across(order[n])] + peer[n]

    settle(0)
    far_up = remote(tile.at[0, low], via.at[0], rs.at[0], rr.at[0], up, orb)
    far_down = remote(tile.at[0, high], via.at[1], rs.at[1], rr.at[1], down, orb)
    far_up.start()
    far_down.start()
    settle(1)
    near_up = remote(tile.at[1, high], last.at[0, high], rs.at[2], rr.at[2], up, orb)
    near_up.start()
    settle(2)
    near_down = remote(tile.at[2, low], last.at[1, low], rs.at[3], rr.at[3], down, orb)
    near_down.start()
    settle(3)
    far_up.wait_recv()
    tile[1, low] += via[0]
    sum_up = remote(tile.at[1, low], last.at[0, low], rs.at[4], rr.at[4], up, orb)
    sum_up.start()
    far_down.wait_recv()
    tile[2, high] += via[1]
    sum_down = remote(tile.at[2, high], last.at[1, high], rs.at[5], rr.at[5], down, orb)
    sum_down.start()
    for copy in (near_up, near_down, sum_up, sum_down):
        copy.wait_recv()
    out_ref[...] = tile[3] + last[0] + last[1]
    for copy in (
        *gather, *spread.values(), *to_x.values(), *to_y.values(), *onward.values(), *swaps,
        far_up, far_down, near_up, near_down, sum_up, sum_down,
    ):
        copy.wait_send()


def direct(half, metric, survive):
    aux_local, occ_local, ao = half.shape
    n_aux, n_orb = lax.axis_size("aux"), lax.axis_size("orb")
    part = occ_local // n_aux
    blocks = gated(half, survive).transpose(1, 0, 2).reshape(n_aux, part * aux_local, ao)
    n_fit = n_aux * aux_local
    width = -(-n_fit // 128) * 128
    metric = jnp.pad(metric, ((0, 0), (0, width - n_fit)))
    depth = n_fit * part
    rows, cols = ao // n_orb, ao // n_aux
    dma = pltpu.SemaphoreType.DMA
    bf16 = jnp.bfloat16
    return pl.pallas_call(
        functools.partial(kernel, aux_local),
        out_shape=jax.ShapeDtypeStruct((rows, cols), F32),
        in_specs=[pl.BlockSpec(memory_space=pltpu.VMEM)] * 2,
        out_specs=pl.BlockSpec(memory_space=pltpu.VMEM),
        scratch_shapes=[
            pltpu.VMEM((4, depth, ao), bf16),
            pltpu.VMEM((depth, ao), bf16),
            pltpu.VMEM((2 * rows, depth), bf16),
            pltpu.VMEM((2 * rows, ao), F32),
            pltpu.VMEM((4, rows, cols), F32),
            pltpu.VMEM((4, rows, cols), F32),
            pltpu.VMEM((2, rows // 2, cols), F32),
            pltpu.VMEM((2, rows, cols), F32),
            pltpu.VMEM((n_fit, width), bf16),
            pltpu.VMEM((depth, depth), bf16),
        ]
        + [dma((4,))] * 12
        + [dma((6,))] * 2,
        compiler_params=pltpu.CompilerParams(
            collective_id=0, has_side_effects=True, vmem_limit_bytes=66 * 1000 * 1000
        ),
    )(blocks, metric)


def solution(mesh):
    square = mesh.shape["aux"] == 4 and mesh.shape["orb"] == 8
    return jax.shard_map(
        direct if square else plain,
        mesh=mesh,
        in_specs=(P("aux", "orb", None), P("aux", None), P("aux", "orb", None)),
        out_specs=P("orb", "aux"),
        check_vma=False,
    )
```

profile of v0, /device:TPU:7, one launch (start us, length us, event | category | flops | bytes accessed | tf_op | source)
XLA Modules:
  0.0 405.3 jit_solution(15822757112344827455)
XLA Ops:
  6.5 0.0 copy-start
  6.5 0.0 all-gather.3.cloned.1.call-start
  6.5 0.7 convert_bitcast_fusion
  7.2 0.1 broadcast_bitcast_fusion
  7.3 3.2 broadcast_multiply_fusion
  10.5 0.0 all-gather.3.cloned.1.call-update
  10.5 0.0 all-gather.5.cloned.1.call-start
  10.6 96.8 %all-gather.3.cloned.1.call-done = bf16[128,24,3072]{2,1,0:T(8,128)(2,1)} async-done(((bf16[16,24,3072]{2,1,0:T(8,128)(2,1)}), bf16[128,24,3072]{2,1,0:T(8,128)(2,1)}) %all-gather.3.cloned.1.call-update) | async-done | bytes 18874384 | tf_op jit(solution)/shard_map/all_gather | solution.py:26
  107.3 17.4 %copy.4 = bf16[16,8,24,3072]{3,1,2,0:T(8,128)(2,1)S(1)} copy(bf16[16,8,24,3072]{3,2,1,0:T(8,128)(2,1)} %bitcast.15) | data formatting | bytes 37748736
  124.8 0.0 copy-done
  124.8 2.7 convolution_convert_fusion
  127.5 2.7 copy.5
  130.2 0.0 all-gather.5.cloned.1.call-update
  130.2 0.0 reduce-scatter.2.cloned.1.call-start
  130.3 218.4 %all-gather.5.cloned.1.call-done = bf16[16,384,3072]{2,1,0:T(8,128)(2,1)} async-done(((bf16[16,24,3072]{2,1,0:T(8,128)(2,1)}), bf16[16,384,3072]{2,1,0:T(8,128)(2,1)}) %all-gather.5.cloned.1.call-update) | async-done | bytes 37748752 | tf_op jit(solution)/shard_map/all_gather | solution.py:31
  348.6 0.0 copy-start.1
  348.6 18.5 %fusion = f32[192,3072]{1,0:T(8,128)} fusion(bf16[6144,3072]{1,0:T(8,128)(2,1)} %bitcast.14, s32[]{:T(128)S(6)} %select_n.3), kind=kOutput, calls=%fused_computation.1 | convolution fusion | flops 7247757312 | bytes 43253764 | tf_op jit(solution)/shard_map/dot_general | solution.py:33
  367.1 0.0 reduce-scatter.2.cloned.1.call-update
  367.1 31.6 %reduce-scatter.2.cloned.1.call-done = f32[192,384]{1,0:T(8,128)} async-done(((f32[192,3072]{1,0:T(8,128)}), f32[192,384]{1,0:T(8,128)}) %reduce-scatter.2.cloned.1.call-update) | async-done | bytes 294928 | tf_op jit(solution)/shard_map/reduce_scatter | solution.py:36
  398.8 0.0 copy-done.1
Async XLA Ops:
  6.5 118.3 %copy-start = (bf16[16,128]{1,0:T(8,128)(2,1)S(1)}, bf16[16,128]{1,0:T(8,128)(2,1)}, u32[]{:S(2)}) copy-start(bf16[16,128]{1,0:T(8,128)(2,1)} %param.4) | copy-start | bytes 12292
  6.5 100.8 %all-gather.3.cloned.1.call-start = ((), (), s32[]{:S(2)}) async-start(), calls=%async_computation.1 | async-start | bytes 21233664 | tf_op jit(solution)/shard_map/all_gather | solution.py:26
  10.5 338.1 %all-gather.5.cloned.1.call-start = ((), (), s32[]{:S(2)}) async-start(), calls=%async_computation.2 | async-start | bytes 40108032 | tf_op jit(solution)/shard_map/all_gather | solution.py:31
  130.2 268.6 %reduce-scatter.2.cloned.1.call-start = ((), (), s32[]{:S(2)}) async-start(), calls=%async_computation.3 | async-start | bytes 2654208 | tf_op jit(solution)/shard_map/reduce_scatter | solution.py:36
  348.6 50.2 %copy-start.1 = (bf16[16,128]{1,0:T(8,128)(2,1)S(1)}, bf16[16,128]{1,0:T(8,128)(2,1)}, u32[]{:S(2)}) copy-start(bf16[16,128]{1,0:T(8,128)(2,1)} %param.4) | copy-start | bytes 12292
Sparse Core Ops, SparseCore 0:
  10.6 96.6 all-gather.2
  130.3 218.2 all-gather.4
  367.3 31.4 reduce-scatter.1
where the time goes:
time: 409 us; the launch traced here: 405 us
  waiting for transfers between devices  347 us (85%)
  matrix products  21.2 us (5%)
  local copies, waits for them, and re-layouts  20.2 us (5%)
  between operations  13.1 us (3%)
    all_gather x1, waiting for transfers between devices, plain(): lax.all_gather(fitted, 'orb', axis=1, tiled=True).reshape(-1, ao_count)  218 us
    all_gather x1, waiting for transfers between devices, plain(): portion = lax.all_gather(gated(half, survive), 'aux', axis=0, tiled=True)  96.8 us
    reduce_scatter x1, waiting for transfers between devices, plain(): return lax.psum_scatter(partial_k, 'aux', scatter_dimension=1, tiled=True)  31.6 us
    unnamed x6, local copies, waits for them, and re-layouts  20.1 us
    dot_general x1, matrix products, plain(): lax.dot_general(left_rows, flat_rows, (((0,), (0,)), ((), ())), preferred...  18.5 us
  transfers between devices with their start and end apart: 3, of which 3 were waited for; matrix products, arithmetic and copies ran while one was open for 0% of the time, Pallas kernels for 0%

commit v1 on v0

v1 whole, which is shorter than its diff:
```python
import jax
import jax.numpy as jnp
from jax import lax
from jax.experimental import pallas as pl
from jax.experimental.pallas import tpu as pltpu
from jax.sharding import PartitionSpec as P

MESH = pl.DeviceIdType.MESH
F32 = jnp.float32


def gated(half, survive):
    aux_local, occ_local, ao_count = half.shape
    blocks_aux, blocks_occ, blocks_ao = survive.shape
    gate = survive.astype(jnp.bfloat16)
    shaped = half.reshape(
        blocks_aux, aux_local, blocks_occ, occ_local // blocks_occ, blocks_ao, ao_count // blocks_ao
    )
    return (shaped * gate[:, None, :, None, :, None]).reshape(aux_local, occ_local, ao_count)


def plain(half, metric, survive):
    aux_local, occ_local, ao_count = half.shape
    portion = lax.all_gather(gated(half, survive), "aux", axis=0, tiled=True)
    fit_total = jnp.dot(metric, portion.reshape(portion.shape[0], -1), preferred_element_type=F32)
    fitted = fit_total.astype(jnp.bfloat16).reshape(aux_local, occ_local, ao_count)
    group_width = ao_count // lax.axis_size("orb")
    row_start = lax.axis_index("orb") * group_width
    flat_rows = lax.all_gather(fitted, "orb", axis=1, tiled=True).reshape(-1, ao_count)
    left_rows = lax.dynamic_slice_in_dim(flat_rows, row_start, group_width, 1)
    partial_k = lax.dot_general(
        left_rows, flat_rows, (((0,), (0,)), ((), ())), preferred_element_type=F32
    )
    return lax.psum_scatter(partial_k, "aux", scatter_dimension=1, tiled=True)


WAVES = (4, 2, 3, 0, 1)


def cube_kernel(
    blocks, metric_ref, out_ref, held, via, whole, fit, turned, left, kf, kb, sb, far1, p1, v, b2, far2, p2,
    ks, fin, acc, mirror, ms, mr, zfs, zfr, zns, znr, zrs, zrr, ds, dr, f1s, f1r, p1s, p1r, f2s, f2r, p2s, p2r,
    zs, zr, xs, xr,
):
    a, o = lax.axis_index("aux"), lax.axis_index("orb")
    z, c = a // 2, a % 2
    x, y = o // 4, o % 4
    ao = blocks.shape[2]
    n_own, part = blocks.shape[1], blocks.shape[0] // 4
    cut = part // 2
    naux = whole.shape[0]
    chunk, cols, rows = ao // 4, ao // 8, ao // 32
    split = rows // 2
    f_step, s_step = 4 - 3 * c, 1 + 3 * c
    f = x * (1 - c) + y * c
    s = y * (1 - c) + x * c
    partner = a + 1 - 2 * c

    def orb_at(df, dsec):
        return ((f + df) % 4) * f_step + ((s + dsec) % 4) * s_step

    def aux_at(dz):
        return ((z + dz) % 4) * 2 + c

    mirrored = z != x
    peers = [(2 * a + h, o // 2) for h in range(2)]
    barrier = pltpu.get_barrier_semaphore()

    def greet(there_a, there_o):
        pl.semaphore_signal(barrier, inc=1, device_id={"aux": there_a, "orb": there_o}, device_id_type=MESH)

    for d in range(1, 8):
        greet((a + d) % 8, o)
    for d in (1, 3):
        greet(a, orb_at(d, 0))
        greet(a, orb_at(0, d))

    @pl.when(mirrored)
    def _():
        for to_o, to_a in peers:
            greet(to_a, to_o)

    pl.semaphore_wait(barrier, 11 + 2 * jnp.where(mirrored, 1, 0))

    def remote(src, dst, send, recv, to_a, to_o):
        return pltpu.make_async_remote_copy(
            src_ref=src, dst_ref=dst, send_sem=send, recv_sem=recv,
            device_id={"aux": to_a, "orb": to_o}, device_id_type=MESH,
        )

    started = []

    def go(copy):
        copy.start()
        started.append(copy)
        return copy

    def aux_rows(aux):
        return pl.ds(pl.multiple_of(aux * n_own, n_own), n_own)

    mine = aux_rows(a)
    span = [pl.ds(k * chunk, chunk) for k in range(4)]

    def orbitals(dz, first, count):
        return pl.ds(((z + dz) % 4) * part + first, count)

    far, near, relay = {}, {}, {}

    def issue(k):
        far[k] = [
            go(remote(blocks.at[orbitals(2, 0, cut), :, span[k]], via.at[0, :, :, span[k]],
                      zfs.at[k, 0], zfr.at[k, 0], aux_at(1), o)),
            go(remote(blocks.at[orbitals(2, cut, cut), :, span[k]], via.at[1, :, :, span[k]],
                      zfs.at[k, 1], zfr.at[k, 1], aux_at(3), o)),
        ]
        near[k] = [
            go(remote(blocks.at[orbitals(dz, 0, part), :, span[k]], held.at[:, mine, span[k]],
                      zns.at[k, n], znr.at[k, n], aux_at(dz), o))
            for n, dz in enumerate((1, 3))
        ]

    issue(0)
    issue(1)
    gather = [
        go(remote(metric_ref, whole.at[mine], ms.at[d], mr.at[d], (a + d) % 8, o)) for d in range(1, 8)
    ]
    own_block = blocks.at[orbitals(0, 0, part)]
    to_partner = {"own": go(remote(own_block, held.at[:, mine], ds.at[12], dr.at[12], partner, o))}
    whole[mine, :] = metric_ref[...]
    held[:, mine, :] = own_block[...]

    def hand_over(k, n, dz):
        there = held.at[:, aux_rows(aux_at(dz)), span[k]]
        to_partner[k, n] = go(remote(there, there, ds.at[3 * k + n], dr.at[3 * k + n], partner, o))

    def finish(k):
        for copy in relay[k]:
            copy.wait_recv()
        hand_over(k, 2, 2)
        if k == 0:
            for copy in gather:
                copy.wait_recv()
            to_partner["own"].wait_recv()
        for n in range(3):
            to_partner[k, n].wait_recv()

        @pl.loop(0, part)
        def _(i):
            at = pl.ds(pl.multiple_of(i * naux, naux), naux)
            fit[at, span[k]] = jnp.dot(
                whole[...], held[i, :, span[k]], preferred_element_type=F32
            ).astype(fit.dtype)

        @pl.loop(0, chunk // 128)
        def _(t):
            at = pl.ds(pl.multiple_of(t * 128, 128), 128)
            src = pl.ds(pl.multiple_of(k * chunk + t * 128, 128), 128)
            turned[at, :] = fit[:, src].T

        for n in range(4):
            at = pl.ds(pl.multiple_of(2 * n * rows + c * rows, rows), rows)
            left[k, n * rows : (n + 1) * rows, :] = turned[at, :]

    for k in range(4):
        for copy in far[k]:
            copy.wait_recv()
        relay[k] = [
            go(remote(via.at[0, :, :, span[k]], held.at[pl.ds(0, cut), aux_rows(aux_at(3)), span[k]],
                      zrs.at[k, 0], zrr.at[k, 0], aux_at(1), o)),
            go(remote(via.at[1, :, :, span[k]], held.at[pl.ds(cut, cut), aux_rows(aux_at(1)), span[k]],
                      zrs.at[k, 1], zrr.at[k, 1], aux_at(3), o)),
        ]
        if k + 2 < 4:
            issue(k + 2)
        for copy in near[k]:
            copy.wait_recv()
        hand_over(k, 0, 3)
        hand_over(k, 1, 1)
        if k:
            finish(k - 1)
    finish(3)

    def multiply(w):
        j = WAVES[w]

        def put(g, first, block):
            at = pl.ds(pl.multiple_of(block * cols, cols), cols)
            count = 4 if j < 4 else 2
            more = jnp.dot(
                left[g, first * rows : (first + count) * rows, :], fit[:, at], preferred_element_type=F32
            )
            for n in range(count):
                tile = more[n * rows : (n + 1) * rows]
                kf[w, 4 * g + first + n] = tile
                kb[w, 4 * g + first + n] = tile.astype(kb.dtype)

        @pl.loop(0, 4)
        def _(g):
            if j < 4:
                put(g, 0, (2 * g + j) % 8)
            else:
                for n in range(2):
                    put(g, 2 * n, 2 * ((g + 2) % 4) + (n + g // 2) % 2)

    first_far, first_in, second_far, second_in, to_owner = {}, {}, {}, {}, {}

    def ring_send(w, src, up, r):
        n = 0 if up else 1
        first_in[w, n, r] = go(remote(
            src, p1.at[w, n, r], p1s.at[w, 4 * n + r], p1r.at[w, 4 * n + r], a, orb_at(1 if up else 3, 0)
        ))

    def stage1(w):
        multiply(w)
        for r in (2, 3, 1, 0):
            up = r in (1, 2)
            first_far[w, r] = go(remote(
                kb.at[w, orb_at(2, r)], far1.at[w, r], f1s.at[w, r], f1r.at[w, r], a, orb_at(1 if up else 3, 0)
            ))
        for r in (2, 3, 1, 0):
            up = r in (0, 3)
            ring_send(w, kb.at[w, orb_at(1 if up else 3, r)], up, r)

    def stage2(w):
        for r in (2, 3, 1, 0):
            up = r in (1, 2)
            first_far[w, r].wait_recv()
            sb[w, r] = (kf[w, orb_at(1 if up else 3, r)] + far1[w, r]).astype(sb.dtype)
            ring_send(w, sb.at[w, r], up, r)

    low, high = pl.ds(0, split), pl.ds(split, split)

    def stage3(w):
        for r in (2, 3, 1, 0):
            first_in[w, 0, r].wait_recv()
            first_in[w, 1, r].wait_recv()
            total = kf[w, orb_at(0, r)] + p1[w, 0, r] + p1[w, 1, r]
            if r == 2:
                b2[w, 0] = total.astype(b2.dtype)
                second_far[w, 0] = go(remote(
                    b2.at[w, 0, low], far2.at[w, 0], f2s.at[w, 0], f2r.at[w, 0], a, orb_at(0, 1)
                ))
                second_far[w, 1] = go(remote(
                    b2.at[w, 0, high], far2.at[w, 1], f2s.at[w, 1], f2r.at[w, 1], a, orb_at(0, 3)
                ))
            else:
                v[w, r] = total

    def stage4(w):
        for n, r in ((0, 1), (1, 3)):
            second_far[w, n].wait_recv()
            summed, plain_rows = (low, high) if n == 0 else (high, low)
            b2[w, 1 + n, summed] = (v[w, r, summed] + far2[w, n]).astype(b2.dtype)
            b2[w, 1 + n, plain_rows] = v[w, r, plain_rows].astype(b2.dtype)
            second_in[w, n] = go(remote(
                b2.at[w, 1 + n], p2.at[w, n], p2s.at[w, n], p2r.at[w, n], a, orb_at(0, r)
            ))

    def owner_of(w):
        j = WAVES[w]
        if j < 4:
            return 2 * ((x + j // 2) % 4) + j % 2
        return 2 * ((x + 2) % 4) + (y // 2 + x // 2) % 2

    def stage5(w):
        for n in range(2):
            second_in[w, n].wait_recv()
        owner = owner_of(w)
        total = v[w, 0] + p2[w, 0] + p2[w, 1]
        d = (owner + 8 - a) % 8
        ks[w] = total
        to_owner[w] = remote(ks.at[w], fin.at[d], zs.at[w], zr.at[d], owner, o)

        @pl.when(owner != a)
        def _():
            to_owner[w].start()

        @pl.when(owner == a)
        def _():
            fin[0] = total

    half_cols = 2 * cols // 3

    def arrive():
        for d in range(1, 8):
            remote(ks.at[0], fin.at[d], zs.at[0], zr.at[d], a, o).wait_recv()
        same = fin[0] + fin[2] + fin[4] + fin[6]
        other = fin[1] + fin[3] + fin[5] + fin[7]
        return same, other

    def place(c_rows):
        return pl.ds(pl.multiple_of(c_rows * rows, rows), rows)

    outgoing = [
        remote(acc.at[:, pl.ds(h * (cols - half_cols), half_cols)], mirror.at[o % 2], xs.at[h], xr.at[o % 2],
               peers[h][1], peers[h][0])
        for h in range(2)
    ]

    def stage6(w):
        j = WAVES[w]

        @pl.when(owner_of(w) == a)
        def _():
            same, other = arrive()
            out_ref[place(c), :] = same
            out_ref[place(1 - c), :] = other
            if j >= 2:
                acc[place(c), :] = same
                acc[place(1 - c), :] = other
                for copy in outgoing:
                    copy.start()

    stages = (stage1, stage2, stage3, stage4, stage5, stage6)
    count = len(WAVES)
    for t in range(count + len(stages) - 1):
        for n, stage in enumerate(stages):
            if 0 <= t - n < count:
                stage(t - n)

    direct = owner_of(0) == a
    for w in range(1, count):
        direct = jnp.logical_or(direct, owner_of(w) == a)
    sent = jnp.logical_and(direct, mirrored)

    @pl.when(jnp.logical_not(direct))
    def _():
        for h in range(2):
            remote(acc.at[:, pl.ds(0, half_cols)], mirror.at[h], xs.at[h], xr.at[h], a, o).wait_recv()
        across = mirror[...].reshape(4 * rows, half_cols).T

        @pl.when(o % 2 == 0)
        def _():
            out_ref[...] = across[: 2 * rows]

        @pl.when(o % 2 == 1)
        def _():
            out_ref[...] = across[half_cols - 2 * rows :]

    for copy in started:
        copy.wait_send()
    for w in range(count):

        @pl.when(owner_of(w) != a)
        def _():
            to_owner[w].wait_send()

    @pl.when(sent)
    def _():
        for copy in outgoing:
            copy.wait_send()


def cube(half, metric, survive):
    aux_local, occ_local, ao = half.shape
    blocks_ao = survive.shape[2]
    gate = jnp.repeat(survive.reshape(blocks_ao).astype(jnp.bfloat16), ao // blocks_ao)
    blocks = (half * gate).transpose(1, 0, 2)
    naux = 8 * aux_local
    part = occ_local // 4
    depth = part * naux
    rows, cols = ao // 32, ao // 8
    waves = len(WAVES)
    dma, vmem = pltpu.SemaphoreType.DMA, pltpu.VMEM
    bf16 = jnp.bfloat16
    return pl.pallas_call(
        cube_kernel,
        out_shape=jax.ShapeDtypeStruct((2 * rows, cols), F32),
        in_specs=[pl.BlockSpec(memory_space=pltpu.VMEM)] * 2,
        out_specs=pl.BlockSpec(memory_space=pltpu.VMEM),
        scratch_shapes=[
            vmem((part, naux, ao), bf16),
            vmem((2, part // 2, aux_local, ao), bf16),
            vmem((naux, naux), bf16),
            vmem((depth, ao), bf16),
            vmem((ao // 4, depth), bf16),
            vmem((4, 4 * rows, depth), bf16),
            vmem((waves, 16, rows, cols), F32),
            vmem((waves, 16, rows, cols), bf16),
            vmem((waves, 4, rows, cols), bf16),
            vmem((waves, 4, rows, cols), bf16),
            vmem((waves, 2, 4, rows, cols), bf16),
            vmem((waves, 4, rows, cols), F32),
            vmem((waves, 3, rows, cols), bf16),
            vmem((waves, 2, rows // 2, cols), bf16),
            vmem((waves, 2, rows, cols), bf16),
            vmem((waves, rows, cols), F32),
            vmem((8, rows, cols), F32),
            vmem((2 * rows, cols), F32),
            vmem((2, 2 * rows, 2 * cols // 3), F32),
        ]
        + [dma((8,))] * 2
        + [dma((4, 2))] * 6
        + [dma((13,))] * 2
        + [dma((waves, 4))] * 2
        + [dma((waves, 8))] * 2
        + [dma((waves, 2))] * 4
        + [dma((waves,)), dma((8,)), dma((2,)), dma((2,))],
        compiler_params=pltpu.CompilerParams(
            collective_id=0, has_side_effects=True, vmem_limit_bytes=66 * 1000 * 1000
        ),
    )(blocks, metric)


def solution(mesh):
    full = mesh.shape["aux"] == 8 and mesh.shape["orb"] == 16
    return jax.shard_map(
        cube if full else plain,
        mesh=mesh,
        in_specs=(P("aux", "orb", None), P("aux", None), P("aux", "orb", None)),
        out_specs=P("orb", "aux"),
        check_vma=False,
    )
```

time: 409 us -> 109 us (0.27)
  the two profiles are of different devices: /device:TPU:7 before, /device:TPU:120 now
where the time goes in v1:
time: 109 us
  Pallas kernels  101 us (93%)
  other arithmetic  6.32 us (6%)
  local copies, waits for them, and re-layouts  1.77 us (2%)
    pallas_call x1, Pallas kernels, cube(): pl.pallas_call(cube_kernel, out_shape=jax.ShapeDtypeStruct((2 * rows, col...  101 us
    transpose x1, other arithmetic, cube(): blocks = (half * gate).transpose(1, 0, 2)  5.66 us

profile of v1, /device:TPU:120, one launch (start us, length us, event | category | flops | bytes accessed | tf_op | source)
XLA Modules:
  0.0 108.9 jit_solution(12230458992946870116)
XLA Ops:
  0.0 0.7 convert_bitcast_fusion
  0.7 0.1 broadcast_bitcast_fusion
  0.7 5.7 %fusion.blocks = bf16[24,16,3072]{2,1,0:T(8,128)(2,1)} fusion(bf16[16,24,3072]{2,1,0:T(8,128)(2,1)} %param.3, bf16[3072]{0:T(1024)(128)(2,1)S(1)} %broadcast_bitcast_fusion), kind=kLoop, calls=%fused_computation.1 | loop fusion | flops 1179648 | bytes 4724736 | tf_op jit(solution)/shard_map/transpose | solution.py:358
  6.4 100.8 %shard_map.37 = f32[192,384]{1,0:T(8,128)} custom-call(bf16[24,16,3072]{2,1,0:T(8,128)(2,1)} %fusion.blocks, bf16[16,128]{1,0:T(8,128)(2,1)} %metric_ref.1), custom_call_target="tpu_custom_call" | custom-call | tf_op jit(solution)/shard_map/pallas_call | solution.py:366
  107.2 1.7 %copy.9 = f32[192,384]{1,0:T(8,128)} copy(f32[192,384]{1,0:T(8,128)} %shard_map.37) | data formatting | bytes 589824

commit v2 on v1

v2 whole, which is shorter than its diff:
```python
import functools

import jax
import jax.numpy as jnp
from jax import lax
from jax.experimental import pallas as pl
from jax.experimental.pallas import tpu as pltpu
from jax.sharding import PartitionSpec as P

MESH = pl.DeviceIdType.MESH
F32 = jnp.float32


def gated(half, survive):
    aux_local, occ_local, ao_count = half.shape
    blocks_aux, blocks_occ, blocks_ao = survive.shape
    gate = survive.astype(jnp.bfloat16)
    shaped = half.reshape(
        blocks_aux, aux_local, blocks_occ, occ_local // blocks_occ, blocks_ao, ao_count // blocks_ao
    )
    return (shaped * gate[:, None, :, None, :, None]).reshape(aux_local, occ_local, ao_count)


def plain(half, metric, survive):
    aux_local, occ_local, ao_count = half.shape
    portion = lax.all_gather(gated(half, survive), "aux", axis=0, tiled=True)
    fit_total = jnp.dot(metric, portion.reshape(portion.shape[0], -1), preferred_element_type=F32)
    fitted = fit_total.astype(jnp.bfloat16).reshape(aux_local, occ_local, ao_count)
    group_width = ao_count // lax.axis_size("orb")
    row_start = lax.axis_index("orb") * group_width
    flat_rows = lax.all_gather(fitted, "orb", axis=1, tiled=True).reshape(-1, ao_count)
    left_rows = lax.dynamic_slice_in_dim(flat_rows, row_start, group_width, 1)
    partial_k = lax.dot_general(
        left_rows, flat_rows, (((0,), (0,)), ((), ())), preferred_element_type=F32
    )
    return lax.psum_scatter(partial_k, "aux", scatter_dimension=1, tiled=True)


WAVES = (
    (0, 0, 0), (0, 1, 0), (0, 2, 1), (1, 3, 0), (0, 0, 1), (1, 1, 0), (2, 2, 2), (1, 3, 1), (1, 0, 1),
)
EARLY = 2
CODES = 32767.0


def side(kind, half_of_x):
    return half_of_x if kind == 2 else kind


def block_at(x, side_of):
    return 2 * x + (x + side_of) % 2


def encode(tile, codes, scale):
    size = jnp.abs(tile)
    lanes = scale.shape[1]
    parts = tile.shape[1] // lanes
    peak = functools.reduce(jnp.maximum, [size[:, n * lanes : (n + 1) * lanes] for n in range(parts)])
    peak = jnp.maximum(jnp.max(peak, axis=0, keepdims=True), 1e-30)
    scale[...] = peak * (1.0 / CODES)
    grow = jnp.concatenate([CODES / peak] * parts, axis=1)
    codes[...] = jnp.round(tile * grow).astype(jnp.int32).astype(codes.dtype)


def decode(codes, scale):
    parts = codes.shape[1] // scale.shape[1]
    grow = jnp.concatenate([scale[...]] * parts, axis=1)
    return codes[...].astype(jnp.int32).astype(F32) * grow


def cube_kernel(
    half_ref, metric_ref, survive_ref, out_ref, raw, pick, blocks, held, via, whole, fit, turned, left,
    kf, q1, c1, far1, cf1, p1, cp1, v, q3, c3, far2, cf2, q4, c4, p2, cp2, ks, fin, acc, mirror,
    ins, ms, mr, zfs, zfr, zns, znr, zrs, zrr, ds, dr, f1s, f1r, p1s, p1r, f2s, f2r, p2s, p2r, zs, zr, xs, xr,
):
    a, o = lax.axis_index("aux"), lax.axis_index("orb")
    z, c = a // 2, a % 2
    x, y = o // 4, o % 4
    ao = fit.shape[1]
    n_own, part = blocks.shape[1], blocks.shape[0] // 4
    cut = part // 2
    naux = whole.shape[0]
    chunk, cols, rows = ao // 4, ao // 8, ao // 32
    split = rows // 2
    f_step, s_step = 4 - 3 * c, 1 + 3 * c
    f = x * (1 - c) + y * c
    s = y * (1 - c) + x * c
    partner = a + 1 - 2 * c

    def at_block(p):
        return pl.ds(p * cols, cols) if isinstance(p, int) else pl.ds(pl.multiple_of(p * cols, cols), cols)

    loads = []
    for p in range(8):
        load = pltpu.make_async_copy(
            half_ref.at[:, at_block(block_at(p % 4, p // 4))], raw.at[:, at_block(p)], ins.at[p]
        )
        load.start()
        loads.append(load)

    def orb_at(df, dsec):
        return ((f + df) % 4) * f_step + ((s + dsec) % 4) * s_step

    def aux_at(dz):
        return ((z + dz) % 4) * 2 + c

    mirrored = o // 2 != a
    peers = [(2 * a + h, o // 2) for h in range(2)]
    barrier = pltpu.get_barrier_semaphore()

    def greet(there_a, there_o):
        pl.semaphore_signal(barrier, inc=1, device_id={"aux": there_a, "orb": there_o}, device_id_type=MESH)

    for d in range(1, 8):
        greet((a + d) % 8, o)
    for d in (1, 3):
        greet(a, orb_at(d, 0))
        greet(a, orb_at(0, d))

    @pl.when(mirrored)
    def _():
        for to_o, to_a in peers:
            greet(to_a, to_o)

    def remote(src, dst, send, recv, to_a, to_o):
        return pltpu.make_async_remote_copy(
            src_ref=src, dst_ref=dst, send_sem=send, recv_sem=recv,
            device_id={"aux": to_a, "orb": to_o}, device_id_type=MESH,
        )

    started = []

    def go(copy):
        copy.start()
        started.append(copy)
        return copy

    depth = raw.shape[0]
    orbs = blocks.shape[0]
    row_of = lax.broadcasted_iota(jnp.int32, (depth, depth), 0)
    col_of = lax.broadcasted_iota(jnp.int32, (depth, depth), 1)
    wanted = lax.rem(row_of, n_own) * orbs + lax.div(row_of, n_own)
    pick[...] = jnp.where(wanted == col_of, 1.0, 0.0).astype(pick.dtype)

    def prepare(k):
        for p in (2 * k, 2 * k + 1):
            loads[p].wait()
            block = block_at(p % 4, p // 4)
            ordered = jnp.dot(pick[...], raw[:, at_block(p)], preferred_element_type=F32)
            for n in range(cols // 128):
                gate = survive_ref[0, block * (cols // 128) + n].astype(F32)
                kept = ordered[:, n * 128 : (n + 1) * 128] * gate
                blocks[:, :, pl.ds(p * cols + n * 128, 128)] = kept.astype(blocks.dtype).reshape(orbs, n_own, 128)

    def aux_rows(aux):
        return pl.ds(pl.multiple_of(aux * n_own, n_own), n_own)

    mine = aux_rows(a)
    span = [pl.ds(k * chunk, chunk) for k in range(4)]

    def orbitals(dz, first, count):
        return pl.ds(((z + dz) % 4) * part + first, count)

    far, near, relay, to_partner = {}, {}, {}, {}

    def issue(k):
        far[k] = [
            go(remote(blocks.at[orbitals(2, 0, cut), :, span[k]], via.at[0, :, :, span[k]],
                      zfs.at[k, 0], zfr.at[k, 0], aux_at(1), o)),
            go(remote(blocks.at[orbitals(2, cut, cut), :, span[k]], via.at[1, :, :, span[k]],
                      zfs.at[k, 1], zfr.at[k, 1], aux_at(3), o)),
        ]
        near[k] = [
            go(remote(blocks.at[orbitals(dz, 0, part), :, span[k]], held.at[:, mine, span[k]],
                      zns.at[k, n], znr.at[k, n], aux_at(dz), o))
            for n, dz in enumerate((1, 3))
        ]
        own = blocks.at[orbitals(0, 0, part), :, span[k]]
        to_partner[k, 3] = go(remote(own, held.at[:, mine, span[k]], ds.at[4 * k + 3], dr.at[4 * k + 3], partner, o))
        held[:, mine, span[k]] = own[...]

    prepare(0)
    pl.semaphore_wait(barrier, 11 + 2 * jnp.where(mirrored, 1, 0))
    issue(0)
    gather = [
        go(remote(metric_ref, whole.at[mine], ms.at[d], mr.at[d], (a + d) % 8, o)) for d in range(1, 8)
    ]
    whole[mine, :] = metric_ref[...]
    prepare(1)
    issue(1)
    prepare(2)
    prepare(3)

    def hand_over(k, n, dz):
        there = held.at[:, aux_rows(aux_at(dz)), span[k]]
        to_partner[k, n] = go(remote(there, there, ds.at[4 * k + n], dr.at[4 * k + n], partner, o))

    def finish(k):
        for copy in relay[k]:
            copy.wait_recv()
        hand_over(k, 2, 2)
        if k == 0:
            for copy in gather:
                copy.wait_recv()
        for n in range(4):
            to_partner[k, n].wait_recv()

        @pl.loop(0, part)
        def _(i):
            at = pl.ds(pl.multiple_of(i * naux, naux), naux)
            fit[at, span[k]] = jnp.dot(
                whole[...], held[i, :, span[k]], preferred_element_type=F32
            ).astype(fit.dtype)

        @pl.loop(0, chunk // 128)
        def _(t):
            at = pl.ds(pl.multiple_of(t * 128, 128), 128)
            src = pl.ds(pl.multiple_of(k * chunk + t * 128, 128), 128)
            turned[at, :] = fit[:, src].T

        for n in range(4):
            at = pl.ds(pl.multiple_of((2 * n + c) * rows, rows), rows)
            left[2 * k + n // 2, (n % 2) * rows : (n % 2 + 1) * rows, :] = turned[at, :]

    def pass_on(k):
        for copy in far[k]:
            copy.wait_recv()
        relay[k] = [
            go(remote(via.at[0, :, :, span[k]], held.at[pl.ds(0, cut), aux_rows(aux_at(3)), span[k]],
                      zrs.at[k, 0], zrr.at[k, 0], aux_at(1), o)),
            go(remote(via.at[1, :, :, span[k]], held.at[pl.ds(cut, cut), aux_rows(aux_at(1)), span[k]],
                      zrs.at[k, 1], zrr.at[k, 1], aux_at(3), o)),
        ]
        if k + 2 < 4:
            issue(k + 2)
        for copy in near[k]:
            copy.wait_recv()
        hand_over(k, 0, 3)
        hand_over(k, 1, 1)

    def target(w, dest, u):
        kind = WAVES[w][0]
        by_x = 2 * ((dest % 2 + side(kind, dest // 2)) % 2) + u
        by_y = 2 * u + (dest // 2 + side(kind, u)) % 2
        return by_x * (1 - c) + by_y * c

    def tile_of(w, df, u):
        dest = (f + df) % 4
        return (2 * dest + u) * (1 - c) + (2 * target(w, dest, u) + dest % 2) * c

    def turn(w, u):
        return (target(w, f, u) + 4 - s) % 4

    def multiply(w):
        rk, step, ck = WAVES[w]

        @pl.loop(0, 4)
        def _(g):
            p = 4 * side(rk, g // 2) + g
            q = 4 * side(ck, g // 2) + (g + step) % 4
            more = jnp.dot(left[p], fit[:, at_block(q)], preferred_element_type=F32)
            kf[w, 2 * g] = more[:rows]
            kf[w, 2 * g + 1] = more[rows:]

    def both(src, src_scale, dst, dst_scale, send, recv, to_o):
        return [
            remote(src, dst, send.at[0], recv.at[0], a, to_o),
            remote(src_scale, dst_scale, send.at[1], recv.at[1], a, to_o),
        ]

    first_far, first_in, second_far, second_in, to_owner = {}, {}, {}, {}, {}

    def ring_send(w, n, u, up):
        d = 0 if up else 1
        first_in[w, u, d] = [go(copy) for copy in both(
            q1.at[w, n], c1.at[w, n], p1.at[w, u, d], cp1.at[w, u, d], p1s.at[w, u, d], p1r.at[w, u, d],
            orb_at(1 if up else 3, 0),
        )]

    def stage1(w):
        multiply(w)
        for u, up in ((0, True), (1, False)):
            encode(kf[w, tile_of(w, 2, u)], q1.at[w, u], c1.at[w, u])
            first_far[w, u] = [go(copy) for copy in both(
                q1.at[w, u], c1.at[w, u], far1.at[w, u], cf1.at[w, u], f1s.at[w, u], f1r.at[w, u],
                orb_at(1 if up else 3, 0),
            )]
        for u, up in ((1, True), (0, False)):
            encode(kf[w, tile_of(w, 1 if up else 3, u)], q1.at[w, 2 + u], c1.at[w, 2 + u])
            ring_send(w, 2 + u, u, up)

    def stage2(w):
        for u, up in ((0, True), (1, False)):
            for copy in first_far[w, u]:
                copy.wait_recv()
            encode(
                kf[w, tile_of(w, 1 if up else 3, u)] + decode(far1.at[w, u], cf1.at[w, u]),
                q1.at[w, 4 + u], c1.at[w, 4 + u],
            )
            ring_send(w, 4 + u, u, up)

    def stage3(w):
        for u in range(2):
            total = kf[w, tile_of(w, 0, u)]
            for d in range(2):
                for copy in first_in[w, u, d]:
                    copy.wait_recv()
                total = total + decode(p1.at[w, u, d], cp1.at[w, u, d])
            v[w, u] = total
            second_far[w, u] = [
                both(
                    q3.at[w, u, pl.ds(d * split, split)], c3.at[w, u], far2.at[w, u], cf2.at[w, u],
                    f2s.at[w, u, d], f2r.at[w, u], orb_at(0, 1 + 2 * d),
                )
                for d in range(2)
            ]

            @pl.when(turn(w, u) == 2)
            def _():
                encode(total, q3.at[w, u], c3.at[w, u])
                for pair in second_far[w, u]:
                    for copy in pair:
                        copy.start()

    def stage4(w):
        for u in range(2):
            r = turn(w, u)
            late = jnp.where(r == 3, 1, 0)
            second_in[w, u] = both(
                q4.at[w, u], c4.at[w, u], p2.at[w, u, late], cp2.at[w, u, late],
                p2s.at[w, u], p2r.at[w, u, late], orb_at(0, r),
            )

            @pl.when(r % 2 == 1)
            def _():
                for copy in second_far[w, u][0]:
                    copy.wait_recv()
                at = pl.ds(pl.multiple_of(late * split, split), split)
                v[w, u, at] += decode(far2.at[w, u], cf2.at[w, u])
                encode(v[w, u], q4.at[w, u], c4.at[w, u])
                for copy in second_in[w, u]:
                    copy.start()

    def owner_of(w):
        step, ck = WAVES[w][1:]
        there = (x + step) % 4
        return 2 * there + (there + side(ck, x // 2)) % 2

    own_side = (x + y // 2) % 2

    def owned(w):
        return jnp.logical_and(own_side == side(WAVES[w][0], x // 2), owner_of(w) == a)

    def stage5(w):
        owner = owner_of(w)
        d = (owner + 8 - a) % 8
        to_owner[w] = remote(ks.at[w], fin.at[d], zs.at[w], zr.at[d], owner, o)
        for u in range(2):

            @pl.when(turn(w, u) == 0)
            def _():
                total = v[w, u]
                for n in range(2):
                    for copy in both(
                        q4.at[w, u], c4.at[w, u], p2.at[w, u, n], cp2.at[w, u, n], p2s.at[w, u], p2r.at[w, u, n], o
                    ):
                        copy.wait_recv()
                    total = total + decode(p2.at[w, u, n], cp2.at[w, u, n])
                ks[w] = total

                @pl.when(owner != a)
                def _():
                    to_owner[w].start()

                @pl.when(owner == a)
                def _():
                    fin[0] = total

    half_cols = 2 * cols // 3

    def place(c_rows):
        return pl.ds(pl.multiple_of(c_rows * rows, rows), rows)

    outgoing = [
        remote(acc.at[:, pl.ds(h * (cols - half_cols), half_cols)], mirror.at[o % 2], xs.at[h], xr.at[o % 2],
               peers[h][1], peers[h][0])
        for h in range(2)
    ]

    def stage6(w):
        @pl.when(owned(w))
        def _():
            for d in range(1, 8):
                remote(ks.at[0], fin.at[d], zs.at[0], zr.at[d], a, o).wait_recv()
            same = fin[0] + fin[2] + fin[4] + fin[6]
            other = fin[1] + fin[3] + fin[5] + fin[7]
            out_ref[place(c), :] = same
            out_ref[place(1 - c), :] = other
            if WAVES[w][1] or WAVES[w][0] != WAVES[w][2]:
                acc[place(c), :] = same
                acc[place(1 - c), :] = other
                for copy in outgoing:
                    copy.start()

    stages = (stage1, stage2, stage3, stage4, stage5, stage6)
    count = len(WAVES)

    for k in range(3):
        pass_on(k)
        if k:
            finish(k - 1)
    for w in range(EARLY):
        stage1(w)
    pass_on(3)
    for w in range(EARLY):
        stage2(w)
    finish(2)
    for w in range(EARLY):
        stage3(w)
    finish(3)
    for t in range(EARLY, count + len(stages) - 1):
        for n, stage in enumerate(stages):
            w = t - n
            if 0 <= w < count and (w >= EARLY or n > 2):
                stage(w)

    direct = functools.reduce(jnp.logical_or, [owned(w) for w in range(count)])

    @pl.when(jnp.logical_not(direct))
    def _():
        for h in range(2):
            remote(acc.at[:, pl.ds(0, half_cols)], mirror.at[h], xs.at[h], xr.at[h], a, o).wait_recv()
        across = mirror[...].reshape(4 * rows, half_cols).T

        @pl.when(o % 2 == 0)
        def _():
            out_ref[...] = across[: 2 * rows]

        @pl.when(o % 2 == 1)
        def _():
            out_ref[...] = across[half_cols - 2 * rows :]

    for copy in started:
        copy.wait_send()
    for w in range(count):
        for u in range(2):
            r = turn(w, u)

            @pl.when(r == 2)
            def _():
                for pair in second_far[w, u]:
                    for copy in pair:
                        copy.wait_send()

            @pl.when(r % 2 == 1)
            def _():
                for copy in second_in[w, u]:
                    copy.wait_send()

            @pl.when(jnp.logical_and(r == 0, owner_of(w) != a))
            def _():
                to_owner[w].wait_send()

    @pl.when(jnp.logical_and(direct, mirrored))
    def _():
        for copy in outgoing:
            copy.wait_send()


def cube(half, metric, survive):
    aux_local, occ_local, ao = half.shape
    naux = 8 * aux_local
    part = occ_local // 4
    depth = part * naux
    own = aux_local * occ_local
    rows, cols = ao // 32, ao // 8
    n = len(WAVES)
    dma, vmem = pltpu.SemaphoreType.DMA, pltpu.VMEM
    bf16, i16 = jnp.bfloat16, jnp.int16

    def coded(*lead, height=rows):
        return [vmem((*lead, height, cols), i16), vmem((*lead, 1, 128), F32)]

    return pl.pallas_call(
        cube_kernel,
        out_shape=jax.ShapeDtypeStruct((2 * rows, cols), F32),
        in_specs=[
            pl.BlockSpec(memory_space=pl.ANY),
            pl.BlockSpec(memory_space=pltpu.VMEM),
            pl.BlockSpec(memory_space=pltpu.SMEM),
        ],
        out_specs=pl.BlockSpec(memory_space=pltpu.VMEM),
        scratch_shapes=[
            vmem((own, ao), bf16),
            vmem((own, own), bf16),
            vmem((occ_local, aux_local, ao), bf16),
            vmem((part, naux, ao), bf16),
            vmem((2, part // 2, aux_local, ao), bf16),
            vmem((naux, naux), bf16),
            vmem((depth, ao), bf16),
            vmem((ao // 4, depth), bf16),
            vmem((8, 2 * rows, depth), bf16),
            vmem((n, 8, rows, cols), F32),
            *coded(n, 6),
            *coded(n, 2),
            *coded(n, 2, 2),
            vmem((n, 2, rows, cols), F32),
            *coded(n, 2),
            *coded(n, 2, height=rows // 2),
            *coded(n, 2),
            *coded(n, 2, 2),
            vmem((n, rows, cols), F32),
            vmem((8, rows, cols), F32),
            vmem((2 * rows, cols), F32),
            vmem((2, 2 * rows, 2 * cols // 3), F32),
        ]
        + [dma((8,))] * 3
        + [dma((4, 2))] * 6
        + [dma((16,))] * 2
        + [dma((n, 2, 2))] * 2
        + [dma((n, 2, 2, 2))] * 2
        + [dma((n, 2, 2, 2)), dma((n, 2, 2))]
        + [dma((n, 2, 2)), dma((n, 2, 2, 2))]
        + [dma((n,)), dma((8,)), dma((2,)), dma((2,))],
        compiler_params=pltpu.CompilerParams(
            collective_id=0, has_side_effects=True, vmem_limit_bytes=66 * 1000 * 1000
        ),
    )(half.reshape(own, ao), metric, survive.reshape(1, -1))


def solution(mesh):
    full = mesh.shape["aux"] == 8 and mesh.shape["orb"] == 16
    return jax.shard_map(
        cube if full else plain,
        mesh=mesh,
        in_specs=(P("aux", "orb", None), P("aux", None), P("aux", "orb", None)),
        out_specs=P("orb", "aux"),
        check_vma=False,
    )
```

time: 109 us -> 113 us (1.037)
  the two profiles are of different devices: /device:TPU:120 before, /device:TPU:7 now
where the time goes in v2:
time: 113 us; the launch traced here: 112 us
  Pallas kernels  110 us (97%)
  local copies, waits for them, and re-layouts  1.69 us (1%)
    pallas_call x1, Pallas kernels, cube(): pl.pallas_call(cube_kernel, out_shape=jax.ShapeDtypeStruct((2 * rows, col...  110 us

profile of v2, /device:TPU:7, one launch (start us, length us, event | category | flops | bytes accessed | tf_op | source)
XLA Modules:
  0.0 111.9 jit_solution(11834008927882476324)
XLA Ops:
  0.0 110.2 %shard_map.37 = f32[192,384]{1,0:T(8,128)} custom-call(bf16[384,3072]{1,0:T(8,128)(2,1)} %bitcast.2, bf16[16,128]{1,0:T(8,128)(2,1)} %metric_ref.1, s32[1,24]{1,0:T(1,128)} %bitcast.3), custom_call_target="tpu_custom_call" | custom-call | tf_op jit(solution)/shard_map/pallas_call | solution.py:484
  110.2 1.7 %copy.5 = f32[192,384]{1,0:T(8,128)} copy(f32[192,384]{1,0:T(8,128)} %shard_map.37) | data formatting | bytes 589824

commit v3 on v2

--- a/solution.py
+++ b/solution.py
@@ -40,6 +40,7 @@
     (0, 0, 0), (0, 1, 0), (0, 2, 1), (1, 3, 0), (0, 0, 1), (1, 1, 0), (2, 2, 2), (1, 3, 1), (1, 0, 1),
 )
 EARLY = 2
+LAGS = (0, 4, 7, 9, 11, 13)
 CODES = 32767.0
 
 
@@ -70,7 +71,8 @@
 
 def cube_kernel(
     half_ref, metric_ref, survive_ref, out_ref, raw, pick, blocks, held, via, whole, fit, turned, left,
-    kf, q1, c1, far1, cf1, p1, cp1, v, q3, c3, far2, cf2, q4, c4, p2, cp2, ks, fin, acc, mirror,
+    kf, q1, c1, far1, cf1, p1, cp1, v, q3, c3, far2, cf2, q4, c4, p2, cp2, ks, cks, fin, cfin, kept, acc, cacc, mirror,
+    cmirror,
     ins, ms, mr, zfs, zfr, zns, znr, zrs, zrr, ds, dr, f1s, f1r, p1s, p1r, f2s, f2r, p2s, p2r, zs, zr, xs, xr,
 ):
     a, o = lax.axis_index("aux"), lax.axis_index("orb")
@@ -117,11 +119,6 @@
         greet(a, orb_at(d, 0))
         greet(a, orb_at(0, d))
 
-    @pl.when(mirrored)
-    def _():
-        for to_o, to_a in peers:
-            greet(to_a, to_o)
-
     def remote(src, dst, send, recv, to_a, to_o):
         return pltpu.make_async_remote_copy(
             src_ref=src, dst_ref=dst, send_sem=send, recv_sem=recv,
@@ -180,7 +177,7 @@
         held[:, mine, span[k]] = own[...]
 
     prepare(0)
-    pl.semaphore_wait(barrier, 11 + 2 * jnp.where(mirrored, 1, 0))
+    pl.semaphore_wait(barrier, 11)
     issue(0)
     gather = [
         go(remote(metric_ref, whole.at[mine], ms.at[d], mr.at[d], (a + d) % 8, o)) for d in range(1, 8)
@@ -354,7 +351,10 @@
     def stage5(w):
         owner = owner_of(w)
         d = (owner + 8 - a) % 8
-        to_owner[w] = remote(ks.at[w], fin.at[d], zs.at[w], zr.at[d], owner, o)
+        to_owner[w] = [
+            remote(ks.at[w], fin.at[d], zs.at[w, 0], zr.at[d, 0], owner, o),
+            remote(cks.at[w], cfin.at[d], zs.at[w, 1], zr.at[d, 1], owner, o),
+        ]
         for u in range(2):
 
             @pl.when(turn(w, u) == 0)
@@ -366,15 +366,16 @@
                     ):
                         copy.wait_recv()
                     total = total + decode(p2.at[w, u, n], cp2.at[w, u, n])
-                ks[w] = total
 
                 @pl.when(owner != a)
                 def _():
-                    to_owner[w].start()
+                    encode(total, ks.at[w], cks.at[w])
+                    for copy in to_owner[w]:
+                        copy.start()
 
                 @pl.when(owner == a)
                 def _():
-                    fin[0] = total
+                    kept[...] = total
 
     half_cols = 2 * cols // 3
 
@@ -382,8 +383,10 @@
         return pl.ds(pl.multiple_of(c_rows * rows, rows), rows)
 
     outgoing = [
-        remote(acc.at[:, pl.ds(h * (cols - half_cols), half_cols)], mirror.at[o % 2], xs.at[h], xr.at[o % 2],
-               peers[h][1], peers[h][0])
+        [
+            remote(acc.at[h], mirror.at[o % 2], xs.at[h, 0], xr.at[o % 2, 0], peers[h][1], peers[h][0]),
+            remote(cacc.at[h], cmirror.at[o % 2], xs.at[h, 1], xr.at[o % 2, 1], peers[h][1], peers[h][0]),
+        ]
         for h in range(2)
     ]
 
@@ -391,16 +394,17 @@
         @pl.when(owned(w))
         def _():
             for d in range(1, 8):
-                remote(ks.at[0], fin.at[d], zs.at[0], zr.at[d], a, o).wait_recv()
-            same = fin[0] + fin[2] + fin[4] + fin[6]
-            other = fin[1] + fin[3] + fin[5] + fin[7]
-            out_ref[place(c), :] = same
-            out_ref[place(1 - c), :] = other
+                remote(ks.at[0], fin.at[d], zs.at[0, 0], zr.at[d, 0], a, o).wait_recv()
+                remote(cks.at[0], cfin.at[d], zs.at[0, 1], zr.at[d, 1], a, o).wait_recv()
+            part_of = [decode(fin.at[d], cfin.at[d]) for d in range(1, 8)]
+            out_ref[place(c), :] = kept[...] + part_of[1] + part_of[3] + part_of[5]
+            out_ref[place(1 - c), :] = part_of[0] + part_of[2] + part_of[4] + part_of[6]
             if WAVES[w][1] or WAVES[w][0] != WAVES[w][2]:
-                acc[place(c), :] = same
-                acc[place(1 - c), :] = other
-                for copy in outgoing:
-                    copy.start()
+                for h in range(2):
+                    encode(out_ref[:, h * (cols - half_cols) : h * (cols - half_cols) + half_cols], acc.at[h], cacc.at[h])
+                for pair in outgoing:
+                    for copy in pair:
+                        copy.start()
 
     stages = (stage1, stage2, stage3, stage4, stage5, stage6)
     count = len(WAVES)
@@ -418,9 +422,9 @@
     for w in range(EARLY):
         stage3(w)
     finish(3)
-    for t in range(EARLY, count + len(stages) - 1):
+    for t in range(EARLY, count + LAGS[-1]):
         for n, stage in enumerate(stages):
-            w = t - n
+            w = t - LAGS[n]
             if 0 <= w < count and (w >= EARLY or n > 2):
                 stage(w)
 
@@ -429,8 +433,9 @@
     @pl.when(jnp.logical_not(direct))
     def _():
         for h in range(2):
-            remote(acc.at[:, pl.ds(0, half_cols)], mirror.at[h], xs.at[h], xr.at[h], a, o).wait_recv()
-        across = mirror[...].reshape(4 * rows, half_cols).T
+            remote(acc.at[h], mirror.at[h], xs.at[h, 0], xr.at[h, 0], a, o).wait_recv()
+            remote(cacc.at[h], cmirror.at[h], xs.at[h, 1], xr.at[h, 1], a, o).wait_recv()
+        across = jnp.concatenate([decode(mirror.at[h], cmirror.at[h]) for h in range(2)], axis=0).T
 
         @pl.when(o % 2 == 0)
         def _():
@@ -459,12 +464,14 @@
 
             @pl.when(jnp.logical_and(r == 0, owner_of(w) != a))
             def _():
-                to_owner[w].wait_send()
+                for copy in to_owner[w]:
+                    copy.wait_send()
 
     @pl.when(jnp.logical_and(direct, mirrored))
     def _():
-        for copy in outgoing:
-            copy.wait_send()
+        for pair in outgoing:
+            for copy in pair:
+                copy.wait_send()
 
 
 def cube(half, metric, survive):
@@ -478,8 +485,8 @@
     dma, vmem = pltpu.SemaphoreType.DMA, pltpu.VMEM
     bf16, i16 = jnp.bfloat16, jnp.int16
 
-    def coded(*lead, height=rows):
-        return [vmem((*lead, height, cols), i16), vmem((*lead, 1, 128), F32)]
+    def coded(*lead, height=rows, width=cols):
+        return [vmem((*lead, height, width), i16), vmem((*lead, 1, 128), F32)]
 
     return pl.pallas_call(
         cube_kernel,
@@ -509,10 +516,11 @@
             *coded(n, 2, height=rows // 2),
             *coded(n, 2),
             *coded(n, 2, 2),
-            vmem((n, rows, cols), F32),
-            vmem((8, rows, cols), F32),
-            vmem((2 * rows, cols), F32),
-            vmem((2, 2 * rows, 2 * cols // 3), F32),
+            *coded(n),
+            *coded(8),
+            vmem((rows, cols), F32),
+            *coded(2, height=2 * rows, width=2 * cols // 3),
+            *coded(2, height=2 * rows, width=2 * cols // 3),
         ]
         + [dma((8,))] * 3
         + [dma((4, 2))] * 6
@@ -521,7 +529,7 @@
         + [dma((n, 2, 2, 2))] * 2
         + [dma((n, 2, 2, 2)), dma((n, 2, 2))]
         + [dma((n, 2, 2)), dma((n, 2, 2, 2))]
-        + [dma((n,)), dma((8,)), dma((2,)), dma((2,))],
+        + [dma((n, 2)), dma((8, 2)), dma((2, 2)), dma((2, 2))],
         compiler_params=pltpu.CompilerParams(
             collective_id=0, has_side_effects=True, vmem_limit_bytes=66 * 1000 * 1000
         ),

time: 113 us -> 95 us (0.84)
  Pallas kernels: 110 us -> 93.1 us
    pallas_call x1, Pallas kernels: 110 us -> 93.1 us  [cube(): pl.pallas_call(cube_kernel, out_shape=jax.ShapeDtypeStruct((2 * rows, col...]
where the time goes in v3:
time: 95 us; the launch traced here: 94.8 us
  Pallas kernels  93.1 us (98%)
  local copies, waits for them, and re-layouts  1.69 us (2%)
    pallas_call x1, Pallas kernels, cube(): pl.pallas_call(cube_kernel, out_shape=jax.ShapeDtypeStruct((2 * rows, col...  93.1 us

profile of v3, /device:TPU:7, one launch (start us, length us, event | category | flops | bytes accessed | tf_op | source)
XLA Modules:
  0.0 94.8 jit_solution(254890527723527632)
XLA Ops:
  0.0 93.1 %shard_map.37 = f32[192,384]{1,0:T(8,128)} custom-call(bf16[384,3072]{1,0:T(8,128)(2,1)} %bitcast.2, bf16[16,128]{1,0:T(8,128)(2,1)} %metric_ref.1, s32[1,24]{1,0:T(1,128)} %bitcast.3), custom_call_target="tpu_custom_call" | custom-call | tf_op jit(solution)/shard_map/pallas_call | solution.py:491
  93.1 1.7 %copy.5 = f32[192,384]{1,0:T(8,128)} copy(f32[192,384]{1,0:T(8,128)} %shard_map.37) | data formatting | bytes 589824

commit v4 on v3

--- a/solution.py
+++ b/solution.py
@@ -37,10 +37,16 @@
 
 
 WAVES = (
-    (0, 0, 0), (0, 1, 0), (0, 2, 1), (1, 3, 0), (0, 0, 1), (1, 1, 0), (2, 2, 2), (1, 3, 1), (1, 0, 1),
+    (0, (0, 0), 0), (0, (1, 1), 0), (0, (0, 2), 1), (1, (3, 3), 0), (0, (2, 0), 1), (1, (1, 1), 0),
+    (2, (2, 2), 2), (1, (3, 3), 1), (1, (0, 0), 1),
 )
-EARLY = 2
-LAGS = (0, 4, 7, 9, 11, 13)
+PLAN = (
+    "r0", "n0", "r1", "n1", "g0", "r2", "q0", "n2", "g1", "r3", "q1", "a0", "n3", "a1",
+    "g2", "g3", "q2", "a2", "b0", "b1", "q3", "a3", "a4", "a5", "b2", "c0", "a6", "b3",
+    "c1", "a7", "b4", "c2", "d0", "a8", "b5", "c3", "d1", "b6", "c4", "d2", "e0", "b7",
+    "c5", "d3", "e1", "b8", "c6", "d4", "e2", "f0", "c7", "d5", "e3", "f1", "c8", "d6",
+    "e4", "f2", "d7", "e5", "f3", "d8", "e6", "f4", "e7", "f5", "e8", "f6", "f7", "f8",
+)
 CODES = 32767.0
 
 
@@ -192,28 +198,24 @@
         there = held.at[:, aux_rows(aux_at(dz)), span[k]]
         to_partner[k, n] = go(remote(there, there, ds.at[4 * k + n], dr.at[4 * k + n], partner, o))
 
-    def finish(k):
+    def gathered(k):
         for copy in relay[k]:
             copy.wait_recv()
         hand_over(k, 2, 2)
+
+    def finish(k):
         if k == 0:
             for copy in gather:
                 copy.wait_recv()
         for n in range(4):
             to_partner[k, n].wait_recv()
 
-        @pl.loop(0, part)
-        def _(i):
-            at = pl.ds(pl.multiple_of(i * naux, naux), naux)
-            fit[at, span[k]] = jnp.dot(
+        for i in range(part):
+            fit[i * naux : (i + 1) * naux, span[k]] = jnp.dot(
                 whole[...], held[i, :, span[k]], preferred_element_type=F32
             ).astype(fit.dtype)
-
-        @pl.loop(0, chunk // 128)
-        def _(t):
-            at = pl.ds(pl.multiple_of(t * 128, 128), 128)
-            src = pl.ds(pl.multiple_of(k * chunk + t * 128, 128), 128)
-            turned[at, :] = fit[:, src].T
+        for t in range(chunk // 128):
+            turned[t * 128 : (t + 1) * 128, :] = fit[:, k * chunk + t * 128 : k * chunk + (t + 1) * 128].T
 
         for n in range(4):
             at = pl.ds(pl.multiple_of((2 * n + c) * rows, rows), rows)
@@ -230,6 +232,8 @@
         ]
         if k + 2 < 4:
             issue(k + 2)
+
+    def take(k):
         for copy in near[k]:
             copy.wait_recv()
         hand_over(k, 0, 3)
@@ -251,10 +255,10 @@
     def multiply(w):
         rk, step, ck = WAVES[w]
 
-        @pl.loop(0, 4)
+        @pl.loop(0, 4, unroll=True)
         def _(g):
             p = 4 * side(rk, g // 2) + g
-            q = 4 * side(ck, g // 2) + (g + step) % 4
+            q = 4 * side(ck, g // 2) + (g + step[0] + (step[1] - step[0]) * (g // 2)) % 4
             more = jnp.dot(left[p], fit[:, at_block(q)], preferred_element_type=F32)
             kf[w, 2 * g] = more[:rows]
             kf[w, 2 * g + 1] = more[rows:]
@@ -340,7 +344,7 @@
 
     def owner_of(w):
         step, ck = WAVES[w][1:]
-        there = (x + step) % 4
+        there = (x + step[0] + (step[1] - step[0]) * (x // 2)) % 4
         return 2 * there + (there + side(ck, x // 2)) % 2
 
     own_side = (x + y // 2) % 2
@@ -399,35 +403,20 @@
             part_of = [decode(fin.at[d], cfin.at[d]) for d in range(1, 8)]
             out_ref[place(c), :] = kept[...] + part_of[1] + part_of[3] + part_of[5]
             out_ref[place(1 - c), :] = part_of[0] + part_of[2] + part_of[4] + part_of[6]
-            if WAVES[w][1] or WAVES[w][0] != WAVES[w][2]:
+            if sum(WAVES[w][1]) or WAVES[w][0] != WAVES[w][2]:
                 for h in range(2):
                     encode(out_ref[:, h * (cols - half_cols) : h * (cols - half_cols) + half_cols], acc.at[h], cacc.at[h])
                 for pair in outgoing:
                     for copy in pair:
                         copy.start()
 
-    stages = (stage1, stage2, stage3, stage4, stage5, stage6)
     count = len(WAVES)
 
-    for k in range(3):
-        pass_on(k)
-        if k:
-            finish(k - 1)
-    for w in range(EARLY):
-        stage1(w)
-    pass_on(3)
-    for w in range(EARLY):
-        stage2(w)
-    finish(2)
-    for w in range(EARLY):
-        stage3(w)
-    finish(3)
-    for t in range(EARLY, count + LAGS[-1]):
-        for n, stage in enumerate(stages):
-            w = t - LAGS[n]
-            if 0 <= w < count and (w >= EARLY or n > 2):
-                stage(w)
-
+    calls = dict(
+        r=pass_on, n=take, g=gathered, q=finish, a=stage1, b=stage2, c=stage3, d=stage4, e=stage5, f=stage6
+    )
+    for name in PLAN:
+        calls[name[0]](int(name[1]))
     direct = functools.reduce(jnp.logical_or, [owned(w) for w in range(count)])
 
     @pl.when(jnp.logical_not(direct))

time: 95 us -> 89.7 us (0.944)
  Pallas kernels: 93.1 us -> 87.8 us
    pallas_call x1, Pallas kernels: 93.1 us -> 87.8 us  [cube(): pl.pallas_call(cube_kernel, out_shape=jax.ShapeDtypeStruct((2 * rows, col...]
where the time goes in v4:
time: 89.7 us; the launch traced here: 89.5 us
  Pallas kernels  87.8 us (98%)
  local copies, waits for them, and re-layouts  1.69 us (2%)
    pallas_call x1, Pallas kernels, cube(): pl.pallas_call(cube_kernel, out_shape=jax.ShapeDtypeStruct((2 * rows, col...  87.8 us

profile of v4, /device:TPU:7, one launch (start us, length us, event | category | flops | bytes accessed | tf_op | source)
XLA Modules:
  0.0 89.5 jit_solution(10587971508728236740)
XLA Ops:
  0.0 87.8 %shard_map.37 = f32[192,384]{1,0:T(8,128)} custom-call(bf16[384,3072]{1,0:T(8,128)(2,1)} %bitcast.2, bf16[16,128]{1,0:T(8,128)(2,1)} %metric_ref.1, s32[1,24]{1,0:T(1,128)} %bitcast.3), custom_call_target="tpu_custom_call" | custom-call | tf_op jit(solution)/shard_map/pallas_call | solution.py:480
  87.8 1.7 %copy.5 = f32[192,384]{1,0:T(8,128)} copy(f32[192,384]{1,0:T(8,128)} %shard_map.37) | data formatting | bytes 589824

commit v5 on v4

--- a/solution.py
+++ b/solution.py
@@ -37,8 +37,8 @@
 
 
 WAVES = (
-    (0, (0, 0), 0), (0, (1, 1), 0), (0, (0, 2), 1), (1, (3, 3), 0), (0, (2, 0), 1), (1, (1, 1), 0),
-    (2, (2, 2), 2), (1, (3, 3), 1), (1, (0, 0), 1),
+    (0, (0, 0), 0), (0, (1, 1), 0), (0, (0, 2), 1), (1, (3, 3), 0), (0, (2, 0), 1),
+    (1, (1, 1), 0), (2, (2, 2), 2), (1, (3, 3), 1), (1, (0, 0), 1),
 )
 PLAN = (
     "r0", "n0", "r1", "n1", "g0", "r2", "q0", "n2", "g1", "r3", "q1", "a0", "n3", "a1",
@@ -79,7 +79,7 @@
     half_ref, metric_ref, survive_ref, out_ref, raw, pick, blocks, held, via, whole, fit, turned, left,
     kf, q1, c1, far1, cf1, p1, cp1, v, q3, c3, far2, cf2, q4, c4, p2, cp2, ks, cks, fin, cfin, kept, acc, cacc, mirror,
     cmirror,
-    ins, ms, mr, zfs, zfr, zns, znr, zrs, zrr, ds, dr, f1s, f1r, p1s, p1r, f2s, f2r, p2s, p2r, zs, zr, xs, xr,
+    ins, bulk, mr, zfr, znr, zrr, dr, f1r, p1r, f2s, f2r, p2s, p2r, zs, zr, xs, xr,
 ):
     a, o = lax.axis_index("aux"), lax.axis_index("orb")
     z, c = a // 2, a % 2
@@ -131,11 +131,8 @@
             device_id={"aux": to_a, "orb": to_o}, device_id_type=MESH,
         )
 
-    started = []
-
     def go(copy):
         copy.start()
-        started.append(copy)
         return copy
 
     depth = raw.shape[0]
@@ -169,24 +166,24 @@
     def issue(k):
         far[k] = [
             go(remote(blocks.at[orbitals(2, 0, cut), :, span[k]], via.at[0, :, :, span[k]],
-                      zfs.at[k, 0], zfr.at[k, 0], aux_at(1), o)),
+                      bulk.at[0], zfr.at[k, 0], aux_at(1), o)),
             go(remote(blocks.at[orbitals(2, cut, cut), :, span[k]], via.at[1, :, :, span[k]],
-                      zfs.at[k, 1], zfr.at[k, 1], aux_at(3), o)),
+                      bulk.at[0], zfr.at[k, 1], aux_at(3), o)),
         ]
         near[k] = [
             go(remote(blocks.at[orbitals(dz, 0, part), :, span[k]], held.at[:, mine, span[k]],
-                      zns.at[k, n], znr.at[k, n], aux_at(dz), o))
+                      bulk.at[0], znr.at[k, n], aux_at(dz), o))
             for n, dz in enumerate((1, 3))
         ]
         own = blocks.at[orbitals(0, 0, part), :, span[k]]
-        to_partner[k, 3] = go(remote(own, held.at[:, mine, span[k]], ds.at[4 * k + 3], dr.at[4 * k + 3], partner, o))
+        to_partner[k, 3] = go(remote(own, held.at[:, mine, span[k]], bulk.at[0], dr.at[4 * k + 3], partner, o))
         held[:, mine, span[k]] = own[...]
 
     prepare(0)
     pl.semaphore_wait(barrier, 11)
     issue(0)
     gather = [
-        go(remote(metric_ref, whole.at[mine], ms.at[d], mr.at[d], (a + d) % 8, o)) for d in range(1, 8)
+        go(remote(metric_ref, whole.at[mine], bulk.at[3], mr.at[d], (a + d) % 8, o)) for d in range(1, 8)
     ]
     whole[mine, :] = metric_ref[...]
     prepare(1)
@@ -196,7 +193,7 @@
 
     def hand_over(k, n, dz):
         there = held.at[:, aux_rows(aux_at(dz)), span[k]]
-        to_partner[k, n] = go(remote(there, there, ds.at[4 * k + n], dr.at[4 * k + n], partner, o))
+        to_partner[k, n] = go(remote(there, there, bulk.at[2], dr.at[4 * k + n], partner, o))
 
     def gathered(k):
         for copy in relay[k]:
@@ -226,9 +223,9 @@
             copy.wait_recv()
         relay[k] = [
             go(remote(via.at[0, :, :, span[k]], held.at[pl.ds(0, cut), aux_rows(aux_at(3)), span[k]],
-                      zrs.at[k, 0], zrr.at[k, 0], aux_at(1), o)),
+                      bulk.at[1], zrr.at[k, 0], aux_at(1), o)),
             go(remote(via.at[1, :, :, span[k]], held.at[pl.ds(cut, cut), aux_rows(aux_at(1)), span[k]],
-                      zrs.at[k, 1], zrr.at[k, 1], aux_at(3), o)),
+                      bulk.at[1], zrr.at[k, 1], aux_at(3), o)),
         ]
         if k + 2 < 4:
             issue(k + 2)
@@ -265,8 +262,8 @@
 
     def both(src, src_scale, dst, dst_scale, send, recv, to_o):
         return [
-            remote(src, dst, send.at[0], recv.at[0], a, to_o),
-            remote(src_scale, dst_scale, send.at[1], recv.at[1], a, to_o),
+            remote(src, dst, send[0], recv.at[0], a, to_o),
+            remote(src_scale, dst_scale, send[1], recv.at[1], a, to_o),
         ]
 
     first_far, first_in, second_far, second_in, to_owner = {}, {}, {}, {}, {}
@@ -274,7 +271,7 @@
     def ring_send(w, n, u, up):
         d = 0 if up else 1
         first_in[w, u, d] = [go(copy) for copy in both(
-            q1.at[w, n], c1.at[w, n], p1.at[w, u, d], cp1.at[w, u, d], p1s.at[w, u, d], p1r.at[w, u, d],
+            q1.at[w, n], c1.at[w, n], p1.at[w, u, d], cp1.at[w, u, d], (bulk.at[4], bulk.at[5]), p1r.at[w, u, d],
             orb_at(1 if up else 3, 0),
         )]
 
@@ -283,7 +280,7 @@
         for u, up in ((0, True), (1, False)):
             encode(kf[w, tile_of(w, 2, u)], q1.at[w, u], c1.at[w, u])
             first_far[w, u] = [go(copy) for copy in both(
-                q1.at[w, u], c1.at[w, u], far1.at[w, u], cf1.at[w, u], f1s.at[w, u], f1r.at[w, u],
+                q1.at[w, u], c1.at[w, u], far1.at[w, u], cf1.at[w, u], (bulk.at[4], bulk.at[5]), f1r.at[w, u],
                 orb_at(1 if up else 3, 0),
             )]
         for u, up in ((1, True), (0, False)):
@@ -311,7 +308,7 @@
             second_far[w, u] = [
                 both(
                     q3.at[w, u, pl.ds(d * split, split)], c3.at[w, u], far2.at[w, u], cf2.at[w, u],
-                    f2s.at[w, u, d], f2r.at[w, u], orb_at(0, 1 + 2 * d),
+                    (f2s.at[w, u, 0, d], f2s.at[w, u, 1, d]), f2r.at[w, u], orb_at(0, 1 + 2 * d),
                 )
                 for d in range(2)
             ]
@@ -329,7 +326,7 @@
             late = jnp.where(r == 3, 1, 0)
             second_in[w, u] = both(
                 q4.at[w, u], c4.at[w, u], p2.at[w, u, late], cp2.at[w, u, late],
-                p2s.at[w, u], p2r.at[w, u, late], orb_at(0, r),
+                (p2s.at[w, u, 0], p2s.at[w, u, 1]), p2r.at[w, u, late], orb_at(0, r),
             )
 
             @pl.when(r % 2 == 1)
@@ -366,7 +363,7 @@
                 total = v[w, u]
                 for n in range(2):
                     for copy in both(
-                        q4.at[w, u], c4.at[w, u], p2.at[w, u, n], cp2.at[w, u, n], p2s.at[w, u], p2r.at[w, u, n], o
+                        q4.at[w, u], c4.at[w, u], p2.at[w, u, n], cp2.at[w, u, n], (p2s.at[w, u, 0], p2s.at[w, u, 1]), p2r.at[w, u, n], o
                     ):
                         copy.wait_recv()
                     total = total + decode(p2.at[w, u, n], cp2.at[w, u, n])
@@ -395,6 +392,20 @@
     ]
 
     def stage6(w):
+        for u in range(2):
+            r = turn(w, u)
+
+            @pl.when(r == 2)
+            def _():
+                for pair in second_far[w, u]:
+                    for copy in pair:
+                        copy.wait_send()
+
+            @pl.when(r % 2 == 1)
+            def _():
+                for copy in second_in[w, u]:
+                    copy.wait_send()
+
         @pl.when(owned(w))
         def _():
             for d in range(1, 8):
@@ -419,6 +430,16 @@
         calls[name[0]](int(name[1]))
     direct = functools.reduce(jnp.logical_or, [owned(w) for w in range(count)])
 
+    sent = (blocks, via, held.at[:, pl.ds(0, 3 * n_own)], whole.at[pl.ds(0, 7 * n_own)], q1, c1)
+    for n, ref in enumerate(sent):
+        remote(ref, ref, bulk.at[n], xr.at[0, 0], a, o).wait_send()
+    for w in range(count):
+
+        @pl.when(jnp.logical_and(jnp.logical_or(turn(w, 0) == 0, turn(w, 1) == 0), owner_of(w) != a))
+        def _():
+            for copy in to_owner[w]:
+                copy.wait_send()
+
     @pl.when(jnp.logical_not(direct))
     def _():
         for h in range(2):
@@ -433,28 +454,6 @@
         @pl.when(o % 2 == 1)
         def _():
             out_ref[...] = across[half_cols - 2 * rows :]
-
-    for copy in started:
-        copy.wait_send()
-    for w in range(count):
-        for u in range(2):
-            r = turn(w, u)
-
-            @pl.when(r == 2)
-            def _():
-                for pair in second_far[w, u]:
-                    for copy in pair:
-                        copy.wait_send()
-
-            @pl.when(r % 2 == 1)
-            def _():
-                for copy in second_in[w, u]:
-                    copy.wait_send()
-
-            @pl.when(jnp.logical_and(r == 0, owner_of(w) != a))
-            def _():
-                for copy in to_owner[w]:
-                    copy.wait_send()
 
     @pl.when(jnp.logical_and(direct, mirrored))
     def _():
@@ -512,10 +511,8 @@
             *coded(2, height=2 * rows, width=2 * cols // 3),
         ]
         + [dma((8,))] * 3
-        + [dma((4, 2))] * 6
-        + [dma((16,))] * 2
-        + [dma((n, 2, 2))] * 2
-        + [dma((n, 2, 2, 2))] * 2
+        + [dma((4, 2))] * 3
+        + [dma((16,)), dma((n, 2, 2)), dma((n, 2, 2, 2))]
         + [dma((n, 2, 2, 2)), dma((n, 2, 2))]
         + [dma((n, 2, 2)), dma((n, 2, 2, 2))]
         + [dma((n, 2)), dma((8, 2)), dma((2, 2)), dma((2, 2))],

time: 89.7 us -> 87.9 us (0.980)
  Pallas kernels: 87.8 us -> 86.1 us
    pallas_call x1, Pallas kernels: 87.8 us -> 86.1 us  [cube(): pl.pallas_call(cube_kernel, out_shape=jax.ShapeDtypeStruct((2 * rows, col...]
where the time goes in v5:
time: 87.9 us; the launch traced here: 87.8 us
  Pallas kernels  86.1 us (98%)
  local copies, waits for them, and re-layouts  1.69 us (2%)
    pallas_call x1, Pallas kernels, cube(): pl.pallas_call(cube_kernel, out_shape=jax.ShapeDtypeStruct((2 * rows, col...  86.1 us

profile of v5, /device:TPU:7, one launch (start us, length us, event | category | flops | bytes accessed | tf_op | source)
XLA Modules:
  0.0 87.8 jit_solution(14190748515368914767)
XLA Ops:
  0.0 86.1 %shard_map.37 = f32[192,384]{1,0:T(8,128)} custom-call(bf16[384,3072]{1,0:T(8,128)(2,1)} %bitcast.2, bf16[16,128]{1,0:T(8,128)(2,1)} %metric_ref.1, s32[1,24]{1,0:T(1,128)} %bitcast.3), custom_call_target="tpu_custom_call" | custom-call | tf_op jit(solution)/shard_map/pallas_call | solution.py:479
  86.1 1.7 %copy.5 = f32[192,384]{1,0:T(8,128)} copy(f32[192,384]{1,0:T(8,128)} %shard_map.37) | data formatting | bytes 589824

commit v6 on v5

--- a/solution.py
+++ b/solution.py
@@ -139,7 +139,8 @@
     orbs = blocks.shape[0]
     row_of = lax.broadcasted_iota(jnp.int32, (depth, depth), 0)
     col_of = lax.broadcasted_iota(jnp.int32, (depth, depth), 1)
-    wanted = lax.rem(row_of, n_own) * orbs + lax.div(row_of, n_own)
+    shift = n_own.bit_length() - 1
+    wanted = jnp.bitwise_and(row_of, n_own - 1) * orbs + jnp.right_shift(row_of, shift)
     pick[...] = jnp.where(wanted == col_of, 1.0, 0.0).astype(pick.dtype)
 
     def prepare(k):
@@ -182,12 +183,12 @@
     prepare(0)
     pl.semaphore_wait(barrier, 11)
     issue(0)
+    prepare(1)
+    issue(1)
     gather = [
         go(remote(metric_ref, whole.at[mine], bulk.at[3], mr.at[d], (a + d) % 8, o)) for d in range(1, 8)
     ]
     whole[mine, :] = metric_ref[...]
-    prepare(1)
-    issue(1)
     prepare(2)
     prepare(3)
 
@@ -415,9 +416,9 @@
             out_ref[place(c), :] = kept[...] + part_of[1] + part_of[3] + part_of[5]
             out_ref[place(1 - c), :] = part_of[0] + part_of[2] + part_of[4] + part_of[6]
             if sum(WAVES[w][1]) or WAVES[w][0] != WAVES[w][2]:
-                for h in range(2):
-                    encode(out_ref[:, h * (cols - half_cols) : h * (cols - half_cols) + half_cols], acc.at[h], cacc.at[h])
-                for pair in outgoing:
+                for h, pair in enumerate(outgoing):
+                    first = h * (cols - half_cols)
+                    encode(out_ref[:, first : first + half_cols], acc.at[h], cacc.at[h])
                     for copy in pair:
                         copy.start()
 

time: 87.9 us -> 87.9 us (level)
  no operation moved by 1% of the time
where the time goes in v6:
time: 87.9 us; the launch traced here: 87.7 us
  Pallas kernels  86 us (98%)
  local copies, waits for them, and re-layouts  1.69 us (2%)
    pallas_call x1, Pallas kernels, cube(): pl.pallas_call(cube_kernel, out_shape=jax.ShapeDtypeStruct((2 * rows, col...  86 us

profile of v6, /device:TPU:7, one launch (start us, length us, event | category | flops | bytes accessed | tf_op | source)
XLA Modules:
  0.0 87.7 jit_solution(12115048748355828885)
XLA Ops:
  0.0 86.0 %shard_map.37 = f32[192,384]{1,0:T(8,128)} custom-call(bf16[384,3072]{1,0:T(8,128)(2,1)} %bitcast.2, bf16[16,128]{1,0:T(8,128)(2,1)} %metric_ref.1, s32[1,24]{1,0:T(1,128)} %bitcast.3), custom_call_target="tpu_custom_call" | custom-call | tf_op jit(solution)/shard_map/pallas_call | solution.py:480
  86.0 1.7 %copy.5 = f32[192,384]{1,0:T(8,128)} copy(f32[192,384]{1,0:T(8,128)} %shard_map.37) | data formatting | bytes 589824
